TPU v7x, 128 devices: a whole 4x4x4 slice. The times are simulated.
128 devices in a mesh: dp: 8 (over z, core), mp: 16 (over x, y).
Axes of the slice: x: 4, y: 4, z: 4, core: 2. Of those that a mesh axis runs over, the one named last changes fastest.
Arguments:
- features: bfloat16 [8192, 2048], P('dp'), may hold values from -21 to 21
- rewards: float32 [32, 256], P('dp'), may hold values from -6 to 6
- old_values: float32 [32, 256], P('dp'), may hold values from -6 to 6
- dones: int32 [32, 256], P('dp'), may hold values 0 or 1
- lengths: int32 [32], P('dp'), may hold values from 128 to 256
- proj_weights: bfloat16 [2048, 2, 8192], P(None, None, 'mp'), may hold values from -0.125 to 0.125
- down_weight: bfloat16 [8192, 2048], P('mp'), may hold values from -0.0625 to 0.0625
- value_head: float32 [2048], replicated, may hold values from -0.0078125 to 0.0078125
- master: float32 [2048, 2, 8192], P('dp', None, 'mp'), may hold values from -0.125 to 0.125
- moment: float32 [2048, 2, 8192], P('dp', None, 'mp'), may hold values from -1.035801e-05 to 1.035801e-05
- second: float32 [2048, 2, 8192], P('dp', None, 'mp'), may hold values from 2.9802322e-13 to 2.9802322e-12
Outputs:
- master_new: float32 [2048, 2, 8192], P('dp', None, 'mp')
- moment_new: float32 [2048, 2, 8192], P('dp', None, 'mp')
- second_new: float32 [2048, 2, 8192], P('dp', None, 'mp')
- working: bfloat16 [2048, 2, 8192], P(None, None, 'mp')
- total_loss: float32 [], replicated
All inputs are finite; a program needn't handle non-finite values. No bound on the sum of `dones` on one device may be relied on, other than what follows from the above.
Results may differ from a plain program's by a relative error of at most 0.0011.
Values may be sent and summed in bfloat16 or wider, within the bound.
A program may use at most 128 MiB of HBM per device.

v0:
```python
import functools
import math
import jax
import jax.numpy as jnp
from jax import lax
from jax.sharding import Mesh
from jax.sharding import PartitionSpec as P

DP = ("dp_0", "dp_1")
MP = ("mp_0", "mp_1")
DP_MP = ("dp_0", "dp_1", "mp_0", "mp_1")
GAMMA = 0.99
LAMBDA = 0.95
MAX_NORM = 0.05


def own_block(parts, axes, sequence):
    shape = [lax.axis_size(a) for a in axes]
    parts = parts.reshape(*shape, *parts.shape[1:])
    parts = parts.transpose(*sequence, *range(len(axes), parts.ndim))
    parts = parts.reshape(-1, *parts.shape[len(axes) :])
    for k in sequence:
        parts = lax.psum_scatter(parts, axes[k], scatter_dimension=0, tiled=True)
    return parts[0]


def in_blocks(value, dim, count):
    before, after = (value.shape[:dim], value.shape[dim + 1 :])
    return jnp.moveaxis(value.reshape(*before, count, -1, *after), dim, 0)


def summed_rows(value, axes, sequence, dim):
    count = lax.axis_size(axes)
    return own_block(in_blocks(value, dim, count), axes, sequence)


def one_axis_at_a_time(value, axes):
    return functools.reduce(lax.psum, axes, value)


def gae_targets(rewards, old_values, dones, lengths):
    seq_len = rewards.shape[1]
    keeps = 1.0 - dones.astype(jnp.float32)
    following = jnp.concatenate([old_values[:, 1:], jnp.zeros_like(old_values[:, :1])], axis=1)
    deltas = rewards + GAMMA * following * keeps - old_values
    counted = jnp.cumsum(dones, axis=1) - dones
    places = jnp.arange(seq_len, dtype=jnp.int32)
    spans = places[None, :] - places[:, None]
    linked = (counted[:, :, None] == counted[:, None, :]) & (spans[None] >= 0)
    powers = jnp.exp(jnp.maximum(spans, 0).astype(jnp.float32) * math.log(GAMMA * LAMBDA))
    kernel = jnp.where(linked, powers[None], jnp.zeros((), jnp.float32))
    advantage = jnp.einsum("ats,as->at", kernel, deltas, precision=lax.Precision.HIGHEST)
    targets = (advantage + old_values).reshape(-1)
    mask = (places[None, :] < lengths[:, None]).astype(jnp.float32).reshape(-1)
    return (targets, mask)


def value_loss(features, mixed, targets, mask, value_head, total_tokens):
    stream = features.astype(jnp.float32) + mixed
    norm_factor = lax.rsqrt(jnp.mean(stream * stream, axis=-1) + 1e-05)
    normed = stream * norm_factor[:, None]
    estimate = jnp.dot(normed, value_head, precision=lax.Precision.HIGHEST)
    errors = estimate - targets
    loss_part = jnp.sum(mask * errors * errors) / total_tokens
    coeff = 2.0 * mask * errors / total_tokens
    head_grad = coeff[:, None] * value_head[None, :]
    out_grad = (
        norm_factor[:, None]
        * (head_grad - normed * jnp.mean(head_grad * normed, axis=-1, keepdims=True))
    ).astype(jnp.bfloat16)
    return (loss_part, out_grad)


def contract_rows(left, right):
    return lax.dot_general(
        left, right, (((0,), (0,)), ((), ())), preferred_element_type=jnp.float32
    )


def per_device(
    features,
    rewards,
    old_values,
    dones,
    lengths,
    proj_weights,
    down_weight,
    value_head,
    master,
    moment,
    second,
):
    token_count = features.shape[0]
    model_width = features.shape[1]
    ff_local = down_weight.shape[0]
    data_ways = lax.axis_size(DP)
    model_ways = lax.axis_size(MP)
    total_tokens = token_count * data_ways
    targets, mask = gae_targets(rewards, old_values, dones, lengths)
    both = jnp.dot(
        features,
        proj_weights.reshape(model_width, 2 * ff_local),
        preferred_element_type=jnp.float32,
    )
    both = both.reshape(token_count, 2, ff_local)
    gate_values = both[:, 0, :]
    up_values = both[:, 1, :]
    hidden = (jax.nn.silu(gate_values) * up_values).astype(jnp.bfloat16)
    mixed = lax.psum(
        jnp.dot(hidden, down_weight, preferred_element_type=jnp.float32).astype(jnp.bfloat16), MP
    ).astype(jnp.float32)
    loss_part, out_grad = value_loss(features, mixed, targets, mask, value_head, total_tokens)
    loss_part = loss_part / model_ways
    hidden_grad = jnp.dot(out_grad, down_weight.T, preferred_element_type=jnp.float32)
    gate_sigmoid = jax.nn.sigmoid(gate_values)
    gate_grad = (
        hidden_grad * up_values * gate_sigmoid * (1.0 + gate_values * (1.0 - gate_sigmoid))
    ).astype(jnp.bfloat16)
    up_grad = (hidden_grad * gate_values * gate_sigmoid).astype(jnp.bfloat16)
    both_grad = jnp.stack([gate_grad, up_grad], axis=1).reshape(token_count, 2 * ff_local)
    row_share = model_width // data_ways
    grads = summed_rows(
        contract_rows(features, both_grad).reshape(row_share * lax.axis_size(DP), 2, ff_local),
        DP,
        (1, 0),
        0,
    )
    squares = jnp.sum(grads * grads)
    squared_total, total_loss = (
        one_axis_at_a_time(squares, DP_MP),
        one_axis_at_a_time(loss_part, DP_MP),
    )
    clip = jnp.minimum(1.0, MAX_NORM / (jnp.sqrt(squared_total) + 1e-06))
    clipped = clip * grads
    moment_new = 0.9 * moment + 0.1 * clipped
    second_new = 0.999 * second + 0.001 * clipped * clipped
    first_hat = moment_new / (1.0 - 0.9**10)
    second_hat = second_new / (1.0 - 0.999**10)
    master_new = master - 0.001 * (first_hat / (jnp.sqrt(second_hat) + 1e-08) + 0.1 * master)
    working = lax.all_gather(master_new.astype(jnp.bfloat16), DP, axis=0, tiled=True)
    return (master_new, moment_new, second_new, working, total_loss)


def solution(mesh):
    finer = Mesh(mesh.devices.reshape(4, 2, 4, 4), ("dp_0", "dp_1", "mp_0", "mp_1"))
    return jax.shard_map(
        per_device,
        mesh=finer,
        in_specs=(
            P(DP, None),
            P(DP, None),
            P(DP, None),
            P(DP, None),
            P(DP),
            P(None, None, MP),
            P(MP, None),
            P(),
            P(DP, None, MP),
            P(DP, None, MP),
            P(DP, None, MP),
        ),
        out_specs=(P(DP, None, MP), P(DP, None, MP), P(DP, None, MP), P(None, None, MP), P()),
        check_vma=False,
    )
```

profile of v0, /device:TPU:1, one launch (start us, length us, event | category | flops | bytes accessed | tf_op | source)
XLA Modules:
  0.0 348.5 jit_solution(17223176488133655442)
XLA Ops:
  7.2 5.5 %copy.34 = bf16[256,8,2,512]{3,1,2,0:T(8,128)(2,1)} copy(bf16[256,8,2,512]{3,2,1,0:T(2,128)(2,1)} %bitcast.73) | data formatting | bytes 8388608
  12.8 6.5 %copy.21 = bf16[1024,2048]{1,0:T(8,128)(2,1)} copy(bf16[1024,2048]{0,1:T(8,128)(2,1)} %bitcast.72) | data formatting | bytes 8388608 | tf_op jit(solution)/shard_map/dot_general | solution.py:100
  19.3 7.6 %fusion.6 = f32[1024,2,512]{0,2,1:T(8,128)S(1)} fusion(bf16[2,512,2048]{2,1,0:T(8,128)(2,1)} %bitcast.74, bf16[1024,2048]{1,0:T(8,128)(2,1)} %param.11), kind=kOutput, calls=%fused_computation.10 | convolution fusion | flops 4294967296 | bytes 12582912 | tf_op jit(solution)/shard_map/dot_general | solution.py:100
  26.9 2.0 copy-done.9
  28.9 4.4 %convolution_convert_fusion = bf16[1024,2048]{1,0:T(8,128)(2,1)} fusion(bf16[512,2048]{1,0:T(8,128)(2,1)S(1)} %copy-done, f32[1024,2,512]{0,2,1:T(8,128)S(1)} %fusion.6), kind=kOutput, calls=%fused_computation.14 | convolution fusion | flops 2152726528 | bytes 10485760 | tf_op jit(solution)/shard_map/dot_general | solution.py:110
  33.6 0.4 copy-done.8
  34.2 1.2 reduce-window.6
  35.9 1.2 fusion.13
  37.1 102.5 %all-reduce.7.cloned.1.call-done = bf16[1024,2048]{1,0:T(8,128)(2,1)} async-done(((bf16[1024,2048]{1,0:T(8,128)(2,1)}), bf16[1024,2048]{1,0:T(8,128)(2,1)}) %all-reduce.7.cloned.1.call-update) | async-done | bytes 4194320 | tf_op jit(solution)/shard_map/psum | solution.py:109
  139.7 5.0 %multiply_reduce_fusion = f32[1024]{0:T(1024)S(1)} fusion(bf16[1024,2048]{1,0:T(8,128)(2,1)} %all-reduce.7.cloned.1.call-done, bf16[1024,2048]{1,0:T(8,128)(2,1)} %param.11), kind=kLoop, calls=%fused_computation.5 | loop fusion | flops 10484736 | bytes 8392704 | tf_op jit(solution)/shard_map/reduce_sum | solution.py:60
  144.7 0.9 copy-done.3
  145.6 8.1 %fusion.4 = f32[1,1024]{1,0:T(1,128)S(1)} fusion(f32[2048,1]{0,1:T(1,128)S(1)} %bitcast.76, bf16[1024,2048]{1,0:T(8,128)(2,1)S(1)} %copy-done.3, bf16[1024,2048]{1,0:T(8,128)(2,1)S(1)} %copy-done.2, f32[1024]{0:T(1024)S(1)} %add_rsqrt_fusion), kind=kOutput, calls=%fused_computation.8 | convolution fusion | flops 33554432 | bytes 8404992 | tf_op jit(solution)/shard_map/dot_general | solution.py:62
  153.7 0.6 fusion.26
  154.4 2.6 fusion
  156.9 5.4 %fusion.19 = (bf16[1024,1,512]{0,2,1:T(8,128)(2,1)S(1)}, bf16[1024,1,512]{0,2,1:T(8,128)(2,1)S(1)}) fusion(f32[1024,2,512]{0,2,1:T(8,128)S(1)} %copy-done.10, bf16[512,2048]{1,0:T(8,128)(2,1)S(1)} %copy-done, bf16[1024,2048]{1,0:T(8,128)(2,1)S(1)} %copy-done.3, bf16[1024,2048]{1,0:T(8,128)(2,1)S(1)} %copy-done.2, f32[1024]{0:T(1024)S(1)} %broadcast_multiply_fusion, ...), kind=kOutput, calls=%fused_computation.36 | convolution fusion | flops 2173173760 | bytes 16797696 | tf_op jit(solution)/shard_map/dot_general | solution.py:114
  162.6 6.7 %convolution_bitcast_fusion = f32[2048,1024]{0,1:T(8,128)} fusion(bf16[1024,1024]{0,1:T(8,128)(2,1)S(1)} %bitcast.75, bf16[1024,2048]{1,0:T(8,128)(2,1)S(1)} %copy-done.2), kind=kOutput, calls=%fused_computation.9 | convolution fusion | flops 4294967296 | bytes 14680064 | tf_op jit(solution)/shard_map/dot_general | solution.py:75
  169.3 11.7 %reshape_reshape_reshape.3 = f32[4,2,256,2,512]{2,1,0,4,3:T(2,128)} reshape(f32[2048,1024]{0,1:T(8,128)} %convolution_bitcast_fusion) | data formatting | bytes 16777216 | tf_op jit(solution)/shard_map/reshape;reshape;reshape | solution.py:19
  181.0 13.1 %copy.24 = f32[2,4,256,2,512]{4,2,3,1,0:T(8,128)} copy(f32[2,4,256,2,512]{2,0,1,4,3:T(2,128)} %bitcast.71) | data formatting | bytes 16777216 | tf_op jit(solution)/shard_map/transpose | solution.py:20
  194.2 19.7 %reduce-scatter.3.cloned.1.call-done = f32[4,256,2,512]{3,1,2,0:T(8,128)} async-done(((f32[8,256,2,512]{3,1,2,0:T(8,128)}), f32[4,256,2,512]{3,1,2,0:T(8,128)}) %reduce-scatter.3.cloned.1.call-update) | async-done | bytes 4194320 | tf_op jit(solution)/shard_map/reduce_scatter | solution.py:23
  214.6 49.8 %reduce-scatter.5.cloned.1.call-done = f32[1,256,2,512]{3,1,2,0:T(8,128)} async-done(((f32[4,256,2,512]{3,1,2,0:T(8,128)}), f32[1,256,2,512]{3,1,2,0:T(8,128)}) %reduce-scatter.5.cloned.1.call-update) | async-done | bytes 1048592 | tf_op jit(solution)/shard_map/reduce_scatter | solution.py:23
  264.4 2.1 multiply_reduce_fusion.1
  266.5 7.1 %all-reduce.3 = (f32[]{:T(128)}, f32[]{:T(128)}) all-reduce(f32[]{:T(128)} %multiply_reduce_fusion.1, f32[]{:T(128)S(6)} %div.55), channel_id=1, replica_groups=mesh['dp_0'=4,'dp_1'=2,'mp_0'=4,'mp_1'=4] {'dp_0'}, use_global_device_ids=true, to_apply=%region_8.9 | all-reduce | flops 2 | bytes 16 | tf_op jit(solution)/shard_map/psum | solution.py:38
  273.6 5.5 %all-reduce.4 = (f32[]{:T(128)}, f32[]{:T(128)}) all-reduce(f32[]{:T(128)} %get-tuple-element.14, f32[]{:T(128)} %get-tuple-element.15), channel_id=1, replica_groups=mesh['dp_0'=4,'dp_1'=2,'mp_0'=4,'mp_1'=4] {'dp_1'}, use_global_device_ids=true, to_apply=%region_9.10 | all-reduce | flops 2 | bytes 16 | tf_op jit(solution)/shard_map/psum | solution.py:38
  279.1 9.0 %all-reduce.2 = (f32[]{:T(128)}, f32[]{:T(128)}) all-reduce(f32[]{:T(128)} %get-tuple-element.16, f32[]{:T(128)} %get-tuple-element.17), channel_id=1, replica_groups=mesh['dp_0'=4,'dp_1'=2,'mp_0'=4,'mp_1'=4] {'mp_0'}, use_global_device_ids=true, to_apply=%region_10.11 | all-reduce | flops 2 | bytes 16 | tf_op jit(solution)/shard_map/psum | solution.py:38
  288.1 9.1 %all-reduce.1 = (f32[]{:T(128)}, f32[]{:T(128)}) all-reduce(f32[]{:T(128)} %get-tuple-element.12, f32[]{:T(128)} %get-tuple-element.13), channel_id=1, replica_groups=mesh['dp_0'=4,'dp_1'=2,'mp_0'=4,'mp_1'=4] {'mp_1'}, use_global_device_ids=true, to_apply=%region_11.12 | all-reduce | flops 2 | bytes 16 | tf_op jit(solution)/shard_map/psum | solution.py:38
  297.9 3.2 fusion.31
  301.1 1.3 copy.28
  302.5 1.8 copy.29
  304.2 1.8 copy.30
  306.0 1.8 copy.31
  307.8 26.3 %all-gather.2.cloned.1.call-done = bf16[2048,2,512]{2,1,0:T(2,128)(2,1)} async-done(((bf16[256,2,512]{2,1,0:T(2,128)(2,1)}), bf16[2048,2,512]{2,1,0:T(2,128)(2,1)}) %all-gather.2.cloned.1.call-update) | async-done | bytes 4194320 | tf_op jit(solution)/shard_map/all_gather | solution.py:140
  334.1 7.8 %copy.53 = bf16[2048,2,512]{2,1,0:T(2,128)(2,1)} copy(bf16[2048,2,512]{2,1,0:T(2,128)(2,1)} %all-gather.2.cloned.1.call-done) | data formatting | bytes 8388608
  (46 shorter events, 1.3 us)
Async XLA Ops:
  7.2 21.7 %copy-start = (bf16[512,2048]{1,0:T(8,128)(2,1)S(1)}, bf16[512,2048]{1,0:T(8,128)(2,1)}, u32[]{:S(2)}) copy-start(bf16[512,2048]{1,0:T(8,128)(2,1)} %param.17) | copy-start | bytes 6291460
  7.2 132.5 %all-reduce.7.cloned.1.call-start = ((), (), s32[]{:S(2)}) async-start(), calls=%async_computation.2 | async-start | bytes 8388608 | tf_op jit(solution)/shard_map/psum | solution.py:109
  26.9 2.0 copy-start.9
  33.3 0.7 copy-start.8
  33.3 0.7 copy-start.5
  33.3 0.8 copy-start.4
  33.3 2.5 copy-start.7
  33.4 180.5 %reduce-scatter.3.cloned.1.call-start = ((), (), s32[]{:S(2)}) async-start(), calls=%async_computation.3 | async-start | bytes 12582912 | tf_op jit(solution)/shard_map/reduce_scatter | solution.py:23
  37.1 107.6 %copy-start.6 = (f32[2048]{0:T(1024)S(1)}, f32[2048]{0:T(1024)}, u32[]{:S(2)}) copy-start(f32[2048]{0:T(1024)} %param.18) | copy-start | bytes 24580
  139.7 5.1 %copy-start.2 = (bf16[1024,2048]{1,0:T(8,128)(2,1)S(1)}, bf16[1024,2048]{1,0:T(8,128)(2,1)}, u32[]{:S(2)}) copy-start(bf16[1024,2048]{1,0:T(8,128)(2,1)} %param.11) | copy-start | bytes 12582916
  139.7 5.9 %copy-start.3 = (bf16[1024,2048]{1,0:T(8,128)(2,1)S(1)}, bf16[1024,2048]{1,0:T(8,128)(2,1)}, u32[]{:S(2)}) copy-start(bf16[1024,2048]{1,0:T(8,128)(2,1)} %all-reduce.7.cloned.1.call-done) | copy-start | bytes 12582916
  154.3 2.6 copy-start.10
  194.1 70.3 %reduce-scatter.5.cloned.1.call-start = ((), (), s32[]{:S(2)}) async-start(), calls=%async_computation.4 | async-start | bytes 5242880 | tf_op jit(solution)/shard_map/reduce_scatter | solution.py:23
  213.9 120.2 %all-gather.2.cloned.1.call-start = ((), (), s32[]{:S(2)}) async-start(), calls=%async_computation.5 | async-start | bytes 4718592 | tf_op jit(solution)/shard_map/all_gather | solution.py:140
  334.1 7.9 %copy-start.1 = (bf16[512,2048]{1,0:T(8,128)(2,1)S(1)}, bf16[512,2048]{1,0:T(8,128)(2,1)}, u32[]{:S(2)}) copy-start(bf16[512,2048]{1,0:T(8,128)(2,1)} %param.17) | copy-start | bytes 6291460
Sparse Core Ops, SparseCore 0:
  33.5 106.1 all-reduce.6
  194.2 19.5 reduce-scatter.2
  216.3 48.0 reduce-scatter.4
  302.6 31.4 all-gather.1
where the time goes:
time: 350 us; the launch traced here: 348 us
  waiting for transfers between devices  198 us (57%)
  local copies, waits for them, and re-layouts  55.1 us (16%)
  matrix products  33.5 us (10%)
  blocking collectives  30.7 us (9%)
  other arithmetic  15.3 us (4%)
  between operations  15.3 us (4%)
    psum x1, waiting for transfers between devices, per_device(): lax.psum(jnp.dot(hidden, down_weight, preferred_element_type=jnp.float32)...  103 us
    reduce_scatter x2, waiting for transfers between devices, own_block(): parts = lax.psum_scatter(parts, axes[k], scatter_dimension=0, tiled=True)  69.5 us
    psum x4, blocking collectives, one_axis_at_a_time(): return functools.reduce(lax.psum, axes, value)  30.7 us
    all_gather x1, waiting for transfers between devices, per_device(): lax.all_gather(master_new.astype(jnp.bfloat16), DP, axis=0, tiled=True)  26.3 us
    unnamed x28, local copies, waits for them, and re-layouts  22 us
    transpose x1, local copies, waits for them, and re-layouts, own_block(): parts = parts.transpose(*sequence, *range(len(axes), parts.ndim))  13.1 us
    another operation x1, local copies, waits for them, and re-layouts, own_block(): parts = parts.reshape(*shape, *parts.shape[1:])  11.7 us
    dot_general x1, matrix products, value_loss(): estimate = jnp.dot(normed, value_head, precision=lax.Precision.HIGHEST)  8.13 us
  transfers between devices with their start and end apart: 4, of which 4 were waited for; matrix products, arithmetic and copies ran while one was open for 2% of the time, Pallas kernels for 0%

commit v1 on v0

--- a/solution.py
+++ b/solution.py
@@ -137,7 +137,10 @@
     first_hat = moment_new / (1.0 - 0.9**10)
     second_hat = second_new / (1.0 - 0.999**10)
     master_new = master - 0.001 * (first_hat / (jnp.sqrt(second_hat) + 1e-08) + 0.1 * master)
-    working = lax.all_gather(master_new.astype(jnp.bfloat16), DP, axis=0, tiled=True)
+    working = jnp.concatenate(
+        lax.all_to_all(jnp.stack([master_new.astype(jnp.bfloat16)] * lax.axis_size(DP)), DP, 0, 0),
+        axis=0,
+    )
     return (master_new, moment_new, second_new, working, total_loss)
 
 

time: 350 us -> 379 us (1.083)
  waiting for transfers between devices: 198 us -> 216 us
  starting transfers between devices: 0.34 us -> 9.1 us
    all_to_all x0 -> x1, waiting for transfers between devices: none -> 43.5 us  [per_device(): lax.all_to_all(jnp.stack([master_new.astype(jnp.bfloat16)] * lax.axis_siz...]
    all_gather x1 -> x0, waiting for transfers between devices: 26.3 us -> none  [per_device(): lax.all_gather(master_new.astype(jnp.bfloat16), DP, axis=0, tiled=True)]
    all_to_all x0 -> x1, starting transfers between devices: none -> 8.8 us  [per_device(): lax.all_to_all(jnp.stack([master_new.astype(jnp.bfloat16)] * lax.axis_siz...]
    another operation x2 -> x3, local copies, waits for them, and re-layouts: 0.1 us -> 4.27 us  [the longest x1 4.17 us: per_device(): jnp.stack([master_new.astype(jnp.bfloat16)] * lax.axis_size(DP))]
where the time goes in v1:
time: 379 us; the launch traced here: 378 us
  waiting for transfers between devices  216 us (57%)
  local copies, waits for them, and re-layouts  58.4 us (15%)
  matrix products  33.5 us (9%)
  blocking collectives  30.7 us (8%)
  other arithmetic  15.3 us (4%)
  between operations  15.3 us (4%)
  starting transfers between devices  9.1 us (2%)
    psum x1, waiting for transfers between devices, per_device(): lax.psum(jnp.dot(hidden, down_weight, preferred_element_type=jnp.float32)...  103 us
    reduce_scatter x2, waiting for transfers between devices, own_block(): parts = lax.psum_scatter(parts, axes[k], scatter_dimension=0, tiled=True)  69.5 us
    all_to_all x1, waiting for transfers between devices, per_device(): lax.all_to_all(jnp.stack([master_new.astype(jnp.bfloat16)] * lax.axis_siz...  43.5 us
    psum x4, blocking collectives, one_axis_at_a_time(): return functools.reduce(lax.psum, axes, value)  30.7 us
    unnamed x28, local copies, waits for them, and re-layouts  22 us
    transpose x1, local copies, waits for them, and re-layouts, own_block(): parts = parts.transpose(*sequence, *range(len(axes), parts.ndim))  13.1 us
    another operation x1, local copies, waits for them, and re-layouts, own_block(): parts = parts.reshape(*shape, *parts.shape[1:])  11.7 us
    all_to_all x1, starting transfers between devices, per_device(): lax.all_to_all(jnp.stack([master_new.astype(jnp.bfloat16)] * lax.axis_siz...  8.8 us
  transfers between devices with their start and end apart: 4, of which 4 were waited for; matrix products, arithmetic and copies ran while one was open for 2% of the time, Pallas kernels for 0%

profile of v1, /device:TPU:1, one launch (start us, length us, event | category | flops | bytes accessed | tf_op | source)
XLA Modules:
  0.0 377.8 jit_solution(431358957323541272)
XLA Ops:
  7.2 5.5 %copy.34 = bf16[256,8,2,512]{3,1,2,0:T(8,128)(2,1)} copy(bf16[256,8,2,512]{3,2,1,0:T(2,128)(2,1)} %bitcast.74) | data formatting | bytes 8388608
  12.8 6.5 %copy.21 = bf16[1024,2048]{1,0:T(8,128)(2,1)} copy(bf16[1024,2048]{0,1:T(8,128)(2,1)} %bitcast.73) | data formatting | bytes 8388608 | tf_op jit(solution)/shard_map/dot_general | solution.py:100
  19.3 7.6 %fusion.6 = f32[1024,2,512]{0,2,1:T(8,128)S(1)} fusion(bf16[2,512,2048]{2,1,0:T(8,128)(2,1)} %bitcast.75, bf16[1024,2048]{1,0:T(8,128)(2,1)} %param.11), kind=kOutput, calls=%fused_computation.10 | convolution fusion | flops 4294967296 | bytes 12582912 | tf_op jit(solution)/shard_map/dot_general | solution.py:100
  26.9 2.0 copy-done.9
  28.9 4.4 %convolution_convert_fusion = bf16[1024,2048]{1,0:T(8,128)(2,1)} fusion(bf16[512,2048]{1,0:T(8,128)(2,1)S(1)} %copy-done, f32[1024,2,512]{0,2,1:T(8,128)S(1)} %fusion.6), kind=kOutput, calls=%fused_computation.14 | convolution fusion | flops 2152726528 | bytes 10485760 | tf_op jit(solution)/shard_map/dot_general | solution.py:110
  34.2 1.2 reduce-window.6
  35.9 1.2 fusion.13
  37.1 102.5 %all-reduce.7.cloned.1.call-done = bf16[1024,2048]{1,0:T(8,128)(2,1)} async-done(((bf16[1024,2048]{1,0:T(8,128)(2,1)}), bf16[1024,2048]{1,0:T(8,128)(2,1)}) %all-reduce.7.cloned.1.call-update) | async-done | bytes 4194320 | tf_op jit(solution)/shard_map/psum | solution.py:109
  139.7 5.0 %multiply_reduce_fusion = f32[1024]{0:T(1024)S(1)} fusion(bf16[1024,2048]{1,0:T(8,128)(2,1)} %all-reduce.7.cloned.1.call-done, bf16[1024,2048]{1,0:T(8,128)(2,1)} %param.11), kind=kLoop, calls=%fused_computation.5 | loop fusion | flops 10484736 | bytes 8392704 | tf_op jit(solution)/shard_map/reduce_sum | solution.py:60
  144.7 0.9 copy-done.3
  145.6 8.1 %fusion.4 = f32[1,1024]{1,0:T(1,128)S(1)} fusion(f32[2048,1]{0,1:T(1,128)S(1)} %bitcast.77, bf16[1024,2048]{1,0:T(8,128)(2,1)S(1)} %copy-done.3, bf16[1024,2048]{1,0:T(8,128)(2,1)S(1)} %copy-done.2, f32[1024]{0:T(1024)S(1)} %add_rsqrt_fusion), kind=kOutput, calls=%fused_computation.8 | convolution fusion | flops 33554432 | bytes 8404992 | tf_op jit(solution)/shard_map/dot_general | solution.py:62
  153.7 0.6 fusion.26
  154.4 2.6 fusion
  156.9 5.4 %fusion.19 = (bf16[1024,1,512]{0,2,1:T(8,128)(2,1)S(1)}, bf16[1024,1,512]{0,2,1:T(8,128)(2,1)S(1)}) fusion(f32[1024,2,512]{0,2,1:T(8,128)S(1)} %copy-done.10, bf16[512,2048]{1,0:T(8,128)(2,1)S(1)} %copy-done, bf16[1024,2048]{1,0:T(8,128)(2,1)S(1)} %copy-done.3, bf16[1024,2048]{1,0:T(8,128)(2,1)S(1)} %copy-done.2, f32[1024]{0:T(1024)S(1)} %broadcast_multiply_fusion, ...), kind=kOutput, calls=%fused_computation.36 | convolution fusion | flops 2173173760 | bytes 16797696 | tf_op jit(solution)/shard_map/dot_general | solution.py:114
  162.6 6.7 %convolution_bitcast_fusion = f32[2048,1024]{0,1:T(8,128)} fusion(bf16[1024,1024]{0,1:T(8,128)(2,1)S(1)} %bitcast.76, bf16[1024,2048]{1,0:T(8,128)(2,1)S(1)} %copy-done.2), kind=kOutput, calls=%fused_computation.9 | convolution fusion | flops 4294967296 | bytes 14680064 | tf_op jit(solution)/shard_map/dot_general | solution.py:75
  169.3 11.7 %reshape_reshape_reshape.3 = f32[4,2,256,2,512]{2,1,0,4,3:T(2,128)} reshape(f32[2048,1024]{0,1:T(8,128)} %convolution_bitcast_fusion) | data formatting | bytes 16777216 | tf_op jit(solution)/shard_map/reshape;reshape;reshape | solution.py:19
  181.0 13.1 %copy.24 = f32[2,4,256,2,512]{4,2,3,1,0:T(8,128)} copy(f32[2,4,256,2,512]{2,0,1,4,3:T(2,128)} %bitcast.72) | data formatting | bytes 16777216 | tf_op jit(solution)/shard_map/transpose | solution.py:20
  194.2 19.7 %reduce-scatter.3.cloned.1.call-done = f32[4,256,2,512]{3,1,2,0:T(8,128)} async-done(((f32[8,256,2,512]{3,1,2,0:T(8,128)}), f32[4,256,2,512]{3,1,2,0:T(8,128)}) %reduce-scatter.3.cloned.1.call-update) | async-done | bytes 4194320 | tf_op jit(solution)/shard_map/reduce_scatter | solution.py:23
  214.5 49.8 %reduce-scatter.5.cloned.1.call-done = f32[1,256,2,512]{3,1,2,0:T(8,128)} async-done(((f32[4,256,2,512]{3,1,2,0:T(8,128)}), f32[1,256,2,512]{3,1,2,0:T(8,128)}) %reduce-scatter.5.cloned.1.call-update) | async-done | bytes 1048592 | tf_op jit(solution)/shard_map/reduce_scatter | solution.py:23
  264.4 2.1 multiply_reduce_fusion.1
  266.5 7.1 %all-reduce.3 = (f32[]{:T(128)}, f32[]{:T(128)}) all-reduce(f32[]{:T(128)} %multiply_reduce_fusion.1, f32[]{:T(128)S(6)} %div.55), channel_id=1, replica_groups=mesh['dp_0'=4,'dp_1'=2,'mp_0'=4,'mp_1'=4] {'dp_0'}, use_global_device_ids=true, to_apply=%region_8.9 | all-reduce | flops 2 | bytes 16 | tf_op jit(solution)/shard_map/psum | solution.py:38
  273.6 5.5 %all-reduce.4 = (f32[]{:T(128)}, f32[]{:T(128)}) all-reduce(f32[]{:T(128)} %get-tuple-element.14, f32[]{:T(128)} %get-tuple-element.15), channel_id=1, replica_groups=mesh['dp_0'=4,'dp_1'=2,'mp_0'=4,'mp_1'=4] {'dp_1'}, use_global_device_ids=true, to_apply=%region_9.10 | all-reduce | flops 2 | bytes 16 | tf_op jit(solution)/shard_map/psum | solution.py:38
  279.1 9.0 %all-reduce.2 = (f32[]{:T(128)}, f32[]{:T(128)}) all-reduce(f32[]{:T(128)} %get-tuple-element.16, f32[]{:T(128)} %get-tuple-element.17), channel_id=1, replica_groups=mesh['dp_0'=4,'dp_1'=2,'mp_0'=4,'mp_1'=4] {'mp_0'}, use_global_device_ids=true, to_apply=%region_10.11 | all-reduce | flops 2 | bytes 16 | tf_op jit(solution)/shard_map/psum | solution.py:38
  288.1 9.1 %all-reduce.1 = (f32[]{:T(128)}, f32[]{:T(128)}) all-reduce(f32[]{:T(128)} %get-tuple-element.12, f32[]{:T(128)} %get-tuple-element.13), channel_id=1, replica_groups=mesh['dp_0'=4,'dp_1'=2,'mp_0'=4,'mp_1'=4] {'mp_1'}, use_global_device_ids=true, to_apply=%region_11.12 | all-reduce | flops 2 | bytes 16 | tf_op jit(solution)/shard_map/psum | solution.py:38
  297.9 3.2 fusion.31
  301.7 4.2 %stack.11 = bf16[8,256,2,512]{3,2,1,0:T(2,128)(2,1)} broadcast(bf16[256,2,512]{2,1,0:T(2,128)(2,1)S(1)} %copy.28), dimensions={1,2,3} | broadcast | bytes 4718592 | tf_op jit(solution)/shard_map/stack | solution.py:141
  305.8 8.8 %all-to-all-start = ((bf16[8,256,2,512]{3,2,1,0:T(2,128)(2,1)}), bf16[8,256,2,512]{3,2,1,0:T(2,128)(2,1)}, u32[]{:S(2)}, u32[]{:S(2)}) async-start(bf16[8,256,2,512]{3,2,1,0:T(2,128)(2,1)} %stack.11), calls=%async_computation.2 | async-start | bytes 8388608 | tf_op jit(solution)/shard_map/all_to_all | solution.py:141
  314.6 1.8 copy.29
  316.4 1.8 copy.30
  318.2 1.8 copy.31
  320.0 43.5 %all-to-all-done = bf16[8,256,2,512]{3,2,1,0:T(2,128)(2,1)} async-done(((bf16[8,256,2,512]{3,2,1,0:T(2,128)(2,1)}), bf16[8,256,2,512]{3,2,1,0:T(2,128)(2,1)}, u32[]{:S(2)}, u32[]{:S(2)}) %all-to-all-start) | async-done | bytes 4194336 | tf_op jit(solution)/shard_map/all_to_all | solution.py:141
  363.4 7.8 %copy.53 = bf16[2048,2,512]{2,1,0:T(2,128)(2,1)} copy(bf16[2048,2,512]{2,1,0:T(2,128)(2,1)} %bitcast.17) | data formatting | bytes 8388608
  (46 shorter events, 2.2 us)
Async XLA Ops:
  7.2 21.7 %copy-start = (bf16[512,2048]{1,0:T(8,128)(2,1)S(1)}, bf16[512,2048]{1,0:T(8,128)(2,1)}, u32[]{:S(2)}) copy-start(bf16[512,2048]{1,0:T(8,128)(2,1)} %param.17) | copy-start | bytes 6291460
  7.2 132.5 %all-reduce.7.cloned.1.call-start = ((), (), s32[]{:S(2)}) async-start(), calls=%async_computation.3 | async-start | bytes 8388608 | tf_op jit(solution)/shard_map/psum | solution.py:109
  26.9 2.0 copy-start.9
  33.3 0.7 copy-start.8
  33.3 0.7 copy-start.5
  33.3 0.8 copy-start.4
  33.3 2.5 copy-start.7
  33.4 180.5 %reduce-scatter.3.cloned.1.call-start = ((), (), s32[]{:S(2)}) async-start(), calls=%async_computation.4 | async-start | bytes 12582912 | tf_op jit(solution)/shard_map/reduce_scatter | solution.py:23
  37.1 107.6 %copy-start.6 = (f32[2048]{0:T(1024)S(1)}, f32[2048]{0:T(1024)}, u32[]{:S(2)}) copy-start(f32[2048]{0:T(1024)} %param.18) | copy-start | bytes 24580
  139.7 5.1 %copy-start.2 = (bf16[1024,2048]{1,0:T(8,128)(2,1)S(1)}, bf16[1024,2048]{1,0:T(8,128)(2,1)}, u32[]{:S(2)}) copy-start(bf16[1024,2048]{1,0:T(8,128)(2,1)} %param.11) | copy-start | bytes 12582916
  139.7 5.9 %copy-start.3 = (bf16[1024,2048]{1,0:T(8,128)(2,1)S(1)}, bf16[1024,2048]{1,0:T(8,128)(2,1)}, u32[]{:S(2)}) copy-start(bf16[1024,2048]{1,0:T(8,128)(2,1)} %all-reduce.7.cloned.1.call-done) | copy-start | bytes 12582916
  154.3 2.6 copy-start.10
  194.1 70.3 %reduce-scatter.5.cloned.1.call-start = ((), (), s32[]{:S(2)}) async-start(), calls=%async_computation.5 | async-start | bytes 5242880 | tf_op jit(solution)/shard_map/reduce_scatter | solution.py:23
  305.8 57.6 %all-to-all-start = ((bf16[8,256,2,512]{3,2,1,0:T(2,128)(2,1)}), bf16[8,256,2,512]{3,2,1,0:T(2,128)(2,1)}, u32[]{:S(2)}, u32[]{:S(2)}) async-start(bf16[8,256,2,512]{3,2,1,0:T(2,128)(2,1)} %stack.11), calls=%async_computation.2 | async-start | bytes 8388608 | tf_op jit(solution)/shard_map/all_to_all | solution.py:141
  363.4 7.9 %copy-start.1 = (bf16[512,2048]{1,0:T(8,128)(2,1)S(1)}, bf16[512,2048]{1,0:T(8,128)(2,1)}, u32[]{:S(2)}) copy-start(bf16[512,2048]{1,0:T(8,128)(2,1)} %param.17) | copy-start | bytes 6291460
Sparse Core Ops, SparseCore 0:
  33.5 106.1 all-reduce.6
  194.2 19.5 reduce-scatter.2
  216.3 48.0 reduce-scatter.4
